TPU v7x, 32 devices: a whole 2x2x4 slice. The times are simulated.
32 devices in a mesh: dp: 4 (over y, core), seq: 8 (over z, x).
Axes of the slice: x: 2, y: 2, z: 4, core: 2. Of those that a mesh axis runs over, the one named last changes fastest.
Arguments:
- tokens: bfloat16 [32768, 2048], P(('dp', 'seq')), parts along dimension 0, may hold values from -6 to 6
- chosen: int32 [4096], P('dp'), parts along dimension 0, may hold values from 0 to 8191, as said below
- gates: float32 [4096], P('dp'), parts along dimension 0, may hold values from 0.5 to 2
- w_query: bfloat16 [2048, 1024], P('seq'), may hold values from -1.8561553 to 1.8561553
- w_key: bfloat16 [2048, 256], P('seq'), may hold values from -0.088388348 to 0.088388348
- w_value: bfloat16 [2048, 256], P('seq'), may hold values from -0.125 to 0.125
- w_out: bfloat16 [1024, 2048], P(None, 'seq'), may hold values from -0.5 to 0.5
Outputs:
- mixed: bfloat16 [32768, 2048], P(('dp', 'seq')), parts along dimension 0
There are 4 independent parts, one for each index of `dp`. A program takes and returns all parts, laid end to end along the dimension named above; an argument that names none is the same for every part. Nothing has to cross between parts.
Inputs may be any that keep to these rules, and one draw needn't show every extreme that they name: `chosen`: distinct positions in increasing order; at most 256 of them lie in one device's 1024 consecutive positions, and exactly 256 lie in some device's positions.
All inputs are finite; a program needn't handle non-finite values.
Results may differ from a plain program's by a relative error of at most 0.006.
Values may be sent and summed in bfloat16 or wider, within the bound.
A program may use at most 128 MiB of HBM per device.

v0:
```python
import math
import jax
import jax.numpy as jnp
from jax import lax
from jax.sharding import PartitionSpec as P

HEADS = 8
KV_HEADS = 2
HEAD_DIM = 128
ROWS_DEV = 128
MOST_OWN = 256
neg_fill = -1e30


def normalize(row_block):
    widened = row_block.astype(jnp.float32)
    scale_rows = lax.rsqrt(jnp.mean(widened * widened, axis=1, keepdims=True) + 1e-06)
    return (widened * scale_rows).astype(jnp.bfloat16)


def per_device(tokens, chosen, gates, w_query, w_key, w_value, w_out):
    shards = lax.axis_size("seq")
    my_index = lax.axis_index("seq")
    tok_rows = tokens.shape[0]
    model_width = tokens.shape[1]
    picked_total = chosen.shape[0]
    slot_count = (MOST_OWN - 1) // shards + 1
    group_size = HEADS // KV_HEADS
    owner_of = chosen // tok_rows
    owners = jnp.arange(shards, dtype=jnp.int32)
    counts = jnp.sum((owner_of[None, :] == owners[:, None]).astype(jnp.int32), axis=1)
    starts = jnp.cumsum(counts) - counts
    my_start = starts[my_index]
    my_count = counts[my_index]
    my_base = my_index * tok_rows
    own_steps = jnp.arange(MOST_OWN, dtype=jnp.int32)
    own_valid = own_steps < my_count
    slot_steps = jnp.arange(slot_count, dtype=jnp.int32)
    lead_step = (owners - my_start) % shards
    offset = lead_step[:, None] + shards * slot_steps[None, :]
    is_valid = offset < my_count
    flat_ids = jnp.clip((my_start + offset).reshape(-1), 0, picked_total - 1)
    flat_valid = is_valid.reshape(-1)
    spot_row = jnp.where(flat_valid, chosen[flat_ids] - my_base, 0)
    row_block = normalize(tokens[spot_row])
    outgoing = jnp.where(flat_valid[:, None], row_block, jnp.zeros_like(row_block)).reshape(
        shards, slot_count, model_width
    )
    arrived = lax.all_to_all(outgoing, "seq", split_axis=0, concat_axis=0, tiled=True)
    local_rows = jnp.arange(ROWS_DEV, dtype=jnp.int32)
    query_order = my_index + shards * local_rows
    source = owner_of[query_order]
    place_at = source * slot_count + (query_order - starts[source]) // shards
    normed = arrived.reshape(shards * slot_count, model_width)[place_at]

    def key_order_of(row_ids):
        return row_ids // ROWS_DEV + shards * (row_ids % ROWS_DEV)

    rows_here = normed.shape[0]
    pieces = (
        lax.all_gather(w_query, "seq", axis=0, tiled=True),
        lax.all_gather(w_key, "seq", axis=0, tiled=True),
        lax.all_gather(w_value, "seq", axis=0, tiled=True),
    )
    query_sum, key_sum, value_sum = tuple(
        (jnp.dot(normed, piece_now, preferred_element_type=jnp.float32) for piece_now in pieces)
    )
    query_matrix = (
        (query_sum * HEAD_DIM ** (-0.5))
        .astype(jnp.bfloat16)
        .reshape(rows_here, KV_HEADS, group_size, HEAD_DIM)
    )
    keys_all = key_sum.astype(jnp.bfloat16)
    values = value_sum.astype(jnp.bfloat16)
    start_state = (
        jnp.full((KV_HEADS, group_size, rows_here), neg_fill, jnp.float32),
        jnp.zeros((KV_HEADS, group_size, rows_here), jnp.float32),
        jnp.zeros((KV_HEADS, group_size, rows_here, HEAD_DIM), jnp.float32),
    )
    key_rows = lax.all_gather(keys_all, "seq", axis=0, tiled=True)
    value_rows = lax.all_gather(values, "seq", axis=0, tiled=True)
    length = key_rows.shape[0]
    block_rows = math.gcd(length, 512)

    def one_block(step_no, inner_state):
        top_score, weight, mixed_sum = inner_state
        first_row = step_no * block_rows
        key_portion = lax.dynamic_slice_in_dim(key_rows, first_row, block_rows, 0).reshape(
            block_rows, KV_HEADS, HEAD_DIM
        )
        value_piece = lax.dynamic_slice_in_dim(value_rows, first_row, block_rows, 0).reshape(
            block_rows, KV_HEADS, HEAD_DIM
        )
        key_order = key_order_of(first_row + jnp.arange(block_rows, dtype=jnp.int32))
        logit_scores = jnp.einsum(
            "qjfh,ujh->jfqu", query_matrix, key_portion, preferred_element_type=jnp.float32
        )
        allowed = key_order[None, :] <= query_order[:, None]
        logit_scores = jnp.where(allowed, logit_scores, neg_fill)
        fresh_top = jnp.maximum(top_score, jnp.max(logit_scores, axis=-1))
        weights_now = jnp.where(allowed, jnp.exp(logit_scores - fresh_top[..., None]), 0.0)
        shrink = jnp.exp(top_score - fresh_top)
        weight = weight * shrink + jnp.sum(weights_now, axis=-1)
        mixed_sum = mixed_sum * shrink[..., None] + jnp.einsum(
            "yoih,hyf->yoif",
            weights_now.astype(jnp.bfloat16),
            value_piece,
            preferred_element_type=jnp.float32,
        )
        return (fresh_top, weight, mixed_sum)

    top_score, weight, mixed_sum = lax.fori_loop(0, length // block_rows, one_block, start_state)
    attended = (
        jnp.transpose(mixed_sum / weight[..., None], (2, 0, 1, 3))
        .reshape(rows_here, HEADS * HEAD_DIM)
        .astype(jnp.bfloat16)
    )
    block_out = jnp.dot(
        attended,
        lax.all_gather(w_out, "seq", axis=1, tiled=True),
        preferred_element_type=jnp.float32,
    ).astype(jnp.bfloat16)
    own_compact = jnp.clip(my_start + own_steps, 0, picked_total - 1)
    slot_steps = jnp.arange(slot_count, dtype=jnp.int32)
    lead_back = (my_index - starts) % shards
    offset_back = lead_back[:, None] + shards * slot_steps[None, :]
    valid_back = offset_back < counts[:, None]
    local_k = jnp.clip((starts[:, None] + offset_back - my_index) // shards, 0, ROWS_DEV - 1)
    outgoing_back = jnp.where(
        valid_back[..., None], block_out[local_k], jnp.zeros((), jnp.bfloat16)
    )
    returned = lax.all_to_all(outgoing_back, "seq", split_axis=0, concat_axis=0, tiled=True)
    pick_at = (my_start + own_steps) % shards * slot_count + jnp.clip(
        own_steps // shards, 0, slot_count - 1
    )
    delta_rows = returned.reshape(shards * slot_count, model_width)[pick_at]
    spot_row = jnp.where(own_valid, chosen[own_compact] - my_base, tok_rows)
    lift_rows = gates[own_compact][:, None] * delta_rows.astype(jnp.float32)
    mixed = tokens.astype(jnp.float32).at[spot_row].add(lift_rows, mode="drop")
    return mixed.astype(jnp.bfloat16)


def solution(mesh):
    return jax.shard_map(
        per_device,
        mesh=mesh,
        in_specs=(
            P(("dp", "seq"), None),
            P("dp"),
            P("dp"),
            P("seq", None),
            P("seq", None),
            P("seq", None),
            P(None, "seq"),
        ),
        out_specs=P(("dp", "seq"), None),
        check_vma=False,
    )
```

profile of v0, /device:TPU:0, one launch (start us, length us, event | category | flops | bytes accessed | tf_op | source)
XLA Modules:
  0.0 318.1 jit_solution(3164678104505626016)
XLA Ops:
  6.5 0.7 all-gather.9.cloned.1.call-update
  7.3 0.0 all-gather.5.cloned.1.call-start
  7.3 0.7 all-gather.5.cloned.1.call-update
  8.0 0.0 all-gather.7.cloned.1.call-start
  8.1 0.7 all-gather.7.cloned.1.call-update
  8.8 0.5 all-gather.11.cloned.1.call-update
  9.3 0.7 add_select_fusion.3
  10.0 0.1 convert_reduce_fusion
  10.2 0.6 dynamic_slice.26
  10.8 0.2 reduce-window.7
  11.0 0.7 fusion.43
  11.6 0.6 and_select_fusion.3
  12.3 0.7 fusion.23
  13.0 0.7 add_compare_fusion.1
  13.6 0.1 lt.196
  13.7 0.1 min.34
  13.8 1.4 gather_fusion.2
  15.3 5.1 %gather_fusion.3 = bf16[256,2048]{1,0:T(8,128)(2,1)S(1)} fusion(bf16[1024,2048]{1,0:T(8,128)(2,1)} %param.9, s32[1024]{0:T(1024)S(1)} %pad_clamp_fusion.4), kind=kCustom, calls=%fused_computation.3 | custom fusion | bytes 2098176 | tf_op jit(solution)/shard_map/gather | solution.py:45
  20.4 0.3 multiply_reduce_fusion
  20.6 0.1 rsqrt.12
  20.7 1.3 fusion.21
  22.0 7.3 %all-to-all-start = ((bf16[8,32,2048]{2,1,0:T(8,128)(2,1)}), bf16[8,32,2048]{2,1,0:T(8,128)(2,1)S(1)}, u32[]{:S(2)}, u32[]{:S(2)}) async-start(bf16[8,32,2048]{2,1,0:T(8,128)(2,1)} %fusion.21), calls=%async_computation | async-start | bytes 2097152 | tf_op jit(solution)/shard_map/all_to_all | solution.py:49
  29.3 1.0 gather_fusion.4
  30.3 0.1 compare_select_fusion
  30.4 0.1 reshape.710
  30.5 4.9 %fusion.40 = s32[128]{0:T(128)S(1)} fusion(s32[128]{0:T(128)S(1)} %gather_fusion.4, s32[]{:T(128)} %bitcast.16, s32[]{:T(128)} %bitcast.17, s32[]{:T(128)} %bitcast.18, s32[]{:T(128)} %bitcast.19, s32[]{:T(128)} %bitcast.20, s32[]{:T(128)} %bitcast.22, s32[]{:T(128)} %bitcast.21, s32[]{:T(128)} %bitcast.15, s32[]{:T(128)} %axis_index.12), kind=kLoop, calls=%fused_computation.132 | loop fusion | flops 5120 | bytes 1060 | tf_op jit(solution)/shard_map/select_n | solution.py:54
  35.5 28.1 %all-to-all-done = bf16[8,32,2048]{2,1,0:T(8,128)(2,1)S(1)} async-done(((bf16[8,32,2048]{2,1,0:T(8,128)(2,1)}), bf16[8,32,2048]{2,1,0:T(8,128)(2,1)S(1)}, u32[]{:S(2)}, u32[]{:S(2)}) %all-to-all-start) | async-done | bytes 1048608 | tf_op jit(solution)/shard_map/all_to_all | solution.py:49
  63.5 0.9 gather_fusion.5
  64.5 1.5 convolution_convert_fusion.1
  66.1 32.1 %all_gather.22 = bf16[1024,256]{1,0:T(8,128)(2,1)S(1)} all-gather(bf16[128,256]{1,0:T(8,128)(2,1)S(1)} %convolution_convert_fusion.1), channel_id=1, replica_groups=mesh['dp'=4,'seq'=8] {'seq'}, dimensions={0}, use_global_device_ids=true | all-gather | bytes 589824 | tf_op jit(solution)/shard_map/all_gather | solution.py:81
  98.2 7.5 %all-gather.5.cloned.1.call-done = bf16[2048,256]{1,0:T(8,128)(2,1)} async-done(((bf16[256,256]{1,0:T(8,128)(2,1)}), bf16[2048,256]{1,0:T(8,128)(2,1)}) %all-gather.5.cloned.1.call-update) | async-done | bytes 1048592 | tf_op jit(solution)/shard_map/all_gather | solution.py:62
  105.7 1.5 convolution_convert_fusion.2
  107.2 33.2 %all_gather.19 = bf16[1024,256]{1,0:T(8,128)(2,1)S(1)} all-gather(bf16[128,256]{1,0:T(8,128)(2,1)S(1)} %convolution_convert_fusion.2), channel_id=1, replica_groups=mesh['dp'=4,'seq'=8] {'seq'}, dimensions={0}, use_global_device_ids=true | all-gather | bytes 589824 | tf_op jit(solution)/shard_map/all_gather | solution.py:80
  140.4 42.1 %all-gather.7.cloned.1.call-done = bf16[2048,1024]{1,0:T(8,128)(2,1)} async-done(((bf16[256,1024]{1,0:T(8,128)(2,1)}), bf16[2048,1024]{1,0:T(8,128)(2,1)}) %all-gather.7.cloned.1.call-update) | async-done | bytes 4194320 | tf_op jit(solution)/shard_map/all_gather | solution.py:61
  182.4 2.9 fusion.20
  185.4 0.2 reshape.642
  185.6 4.9 %while.20 = (s32[]{:T(128)}, f32[2,4,128]{2,1,0:T(4,128)S(1)}, f32[2,4,128]{2,1,0:T(4,128)S(1)}, f32[2,4,128,128]{3,2,1,0:T(8,128)S(1)}, bf16[1024,256]{1,0:T(8,...) while((s32[]{:T(128)}, f32[2,4,128]{2,1,0:T(4,128)S(1)}, ...), condition=%wide.region_6.7_spmd.clone, body=%wide.region_3.6_spmd.clone.sunk | while | flops 274153728 | bytes 10556611 | solution.py:112
  185.7 0.1 broadcast_compare_fusion.2
  185.9 0.1 copy.35
  186.0 0.1 copy.36
  186.2 0.5 fusion.68
  186.7 0.4 fusion.69
  187.1 0.9 convolution_add_fusion.2
  188.1 0.1 broadcast_compare_fusion.2
  188.3 0.1 copy.35
  188.5 0.1 copy.36
  188.6 0.5 fusion.68
  189.1 0.4 fusion.69
  189.6 0.9 convolution_add_fusion.2
  190.5 0.2 copy.23
  190.7 0.1 divide_convert_fusion
  190.8 66.8 %all-gather.11.cloned.1.call-done = bf16[1024,2048]{1,0:T(8,128)(2,1)} async-done(((bf16[1024,256]{1,0:T(8,128)(2,1)}), bf16[1024,2048]{1,0:T(8,128)(2,1)}) %all-gather.11.cloned.1.call-update) | async-done | bytes 4194320 | tf_op jit(solution)/shard_map/all_gather | solution.py:120
  257.5 2.9 convolution_convert_fusion
  260.5 1.4 gather_fusion.6
  261.8 1.1 broadcast_select_fusion
  262.9 3.7 %all-to-all-start.1 = ((bf16[8,32,2048]{2,1,0:T(8,128)(2,1)}), bf16[8,32,2048]{2,1,0:T(8,128)(2,1)S(1)}, u32[]{:S(2)}, u32[]{:S(2)}) async-start(bf16[8,32,2048]{2,1,0:T(8,128)(2,1)} %broadcast_select_fusion), calls=%async_computation.1 | async-start | bytes 2097152 | tf_op jit(solution)/shard_map/all_to_all | solution.py:132
  266.7 6.5 %convert_element_type.56 = f32[1024,2048]{1,0:T(8,128)} convert(bf16[1024,2048]{1,0:T(8,128)(2,1)} %param.9) | non-fusion elementwise | flops 2097152 | bytes 12582912 | tf_op jit(solution)/shard_map/convert_element_type | solution.py:139
  273.2 0.6 compare_select_fusion.1
  273.8 1.4 gather_fusion
  275.2 1.4 gather_fusion.1
  276.6 0.6 compare_select_fusion.4
  277.3 14.5 %all-to-all-done.1 = bf16[8,32,2048]{2,1,0:T(8,128)(2,1)S(1)} async-done(((bf16[8,32,2048]{2,1,0:T(8,128)(2,1)}), bf16[8,32,2048]{2,1,0:T(8,128)(2,1)S(1)}, u32[]{:S(2)}, u32[]{:S(2)}) %all-to-all-start.1) | async-done | bytes 1048608 | tf_op jit(solution)/shard_map/all_to_all | solution.py:132
  291.7 13.8 %scatter_custom_fusion = f32[1024,2048]{1,0:T(8,128)} fusion(f32[1024,2048]{1,0:T(8,128)} %convert_element_type.56, s32[256]{0:T(256)S(1)} %bitcast.130, f32[256]{0:T(256)S(1)} %gather_fusion.1, bf16[256,2048]{1,0:T(8,128)(2,1)S(1)} %bitcast.120, s32[1024]{0:T(1024)S(1)} %pad_clamp_fusion), kind=kCustom, calls=%fused_computation.43 | custom fusion | flops 1572864 | bytes 9442304 | tf_op jit(solution)/shard_map/scatter-add | solution.py:139
  305.5 6.0 %convert_element_type.70 = bf16[1024,2048]{1,0:T(8,128)(2,1)} convert(f32[1024,2048]{1,0:T(8,128)} %scatter_custom_fusion) | non-fusion elementwise | flops 2097152 | bytes 12582912 | tf_op jit(solution)/shard_map/convert_element_type | solution.py:140
  (38 shorter events, 0.4 us)
Async XLA Ops:
  6.5 268.7 %copy-start = (f32[1024]{0:T(1024)S(1)}, f32[1024]{0:T(1024)}, u32[]{:S(2)}) copy-start(f32[1024]{0:T(1024)} %param.11) | copy-start | bytes 12292
  6.5 7.3 %copy-start.1 = (s32[1024]{0:T(1024)S(1)}, s32[1024]{0:T(1024)}, u32[]{:S(2)}) copy-start(s32[1024]{0:T(1024)} %param.10) | copy-start | bytes 12292
  6.5 58.0 %all-gather.9.cloned.1.call-start = ((), (), s32[]{:S(2)}) async-start(), calls=%async_computation.4 | async-start | bytes 1179648 | tf_op jit(solution)/shard_map/all_gather | solution.py:63
  7.3 98.4 %all-gather.5.cloned.1.call-start = ((), (), s32[]{:S(2)}) async-start(), calls=%async_computation.2 | async-start | bytes 1179648 | tf_op jit(solution)/shard_map/all_gather | solution.py:62
  8.0 174.4 %all-gather.7.cloned.1.call-start = ((), (), s32[]{:S(2)}) async-start(), calls=%async_computation.3 | async-start | bytes 4718592 | tf_op jit(solution)/shard_map/all_gather | solution.py:61
  8.7 248.8 %all-gather.11.cloned.1.call-start = ((), (), s32[]{:S(2)}) async-start(), calls=%async_computation.5 | async-start | bytes 4718592 | tf_op jit(solution)/shard_map/all_gather | solution.py:120
  22.0 41.5 %all-to-all-start = ((bf16[8,32,2048]{2,1,0:T(8,128)(2,1)}), bf16[8,32,2048]{2,1,0:T(8,128)(2,1)S(1)}, u32[]{:S(2)}, u32[]{:S(2)}) async-start(bf16[8,32,2048]{2,1,0:T(8,128)(2,1)} %fusion.21), calls=%async_computation | async-start | bytes 2097152 | tf_op jit(solution)/shard_map/all_to_all | solution.py:49
  262.9 28.8 %all-to-all-start.1 = ((bf16[8,32,2048]{2,1,0:T(8,128)(2,1)}), bf16[8,32,2048]{2,1,0:T(8,128)(2,1)S(1)}, u32[]{:S(2)}, u32[]{:S(2)}) async-start(bf16[8,32,2048]{2,1,0:T(8,128)(2,1)} %broadcast_select_fusion), calls=%async_computation.1 | async-start | bytes 2097152 | tf_op jit(solution)/shard_map/all_to_all | solution.py:132
Sparse Core Ops, SparseCore 0:
  9.5 53.3 all-gather.8
  65.0 40.6 all-gather.4
  107.8 74.5 all-gather.6
  184.3 73.1 all-gather.10
where the time goes:
time: 319 us; the launch traced here: 318 us
  waiting for transfers between devices  161 us (50%)
  blocking collectives  65.3 us (20%)
  other arithmetic  39.7 us (12%)
  local copies, waits for them, and re-layouts  15.1 us (5%)
  between operations  13.4 us (4%)
  matrix products  11.8 us (4%)
  starting transfers between devices  11.1 us (3%)
    all_gather x1, waiting for transfers between devices, per_device(): lax.all_gather(w_out, 'seq', axis=1, tiled=True)  66.8 us
    all_gather x1, waiting for transfers between devices, per_device(): lax.all_gather(w_query, 'seq', axis=0, tiled=True)  42.1 us
    all_gather x1, blocking collectives, per_device(): key_rows = lax.all_gather(keys_all, 'seq', axis=0, tiled=True)  33.2 us
    all_gather x1, blocking collectives, per_device(): value_rows = lax.all_gather(values, 'seq', axis=0, tiled=True)  32.1 us
    all_to_all x1, waiting for transfers between devices, per_device(): lax.all_to_all(outgoing, 'seq', split_axis=0, concat_axis=0, tiled=True)  28.1 us
    all_to_all x1, waiting for transfers between devices, per_device(): lax.all_to_all(outgoing_back, 'seq', split_axis=0, concat_axis=0, tiled=T...  14.5 us
    scatter-add x1, other arithmetic, per_device(): mixed = tokens.astype(jnp.float32).at[spot_row].add(lift_rows, mode='drop')  13.8 us
    all_gather x1, waiting for transfers between devices, per_device(): lax.all_gather(w_key, 'seq', axis=0, tiled=True)  7.47 us
  transfers between devices with their start and end apart: 6, of which 5 were waited for; matrix products, arithmetic and copies ran while one was open for 13% of the time, Pallas kernels for 0%

commit v1 on v0

--- a/solution.py
+++ b/solution.py
@@ -117,7 +117,7 @@
     )
     block_out = jnp.dot(
         attended,
-        lax.all_gather(w_out, "seq", axis=1, tiled=True),
+        jnp.concatenate(lax.all_gather(w_out, "seq"), axis=1),
         preferred_element_type=jnp.float32,
     ).astype(jnp.bfloat16)
     own_compact = jnp.clip(my_start + own_steps, 0, picked_total - 1)

time: 319 us -> 327 us (1.025)
  local copies, waits for them, and re-layouts: 15.1 us -> 21.6 us
    all_gather x1, waiting for transfers between devices: 42.1 us -> 66.9 us  [per_device(): lax.all_gather(w_query, 'seq', axis=0, tiled=True)]
    all_gather x1, waiting for transfers between devices: 66.8 us -> 41.9 us  [per_device(): lax.all_gather(w_out, 'seq')]
    reshape x0 -> x1, local copies, waits for them, and re-layouts: none -> 6.42 us  [per_device(): jnp.concatenate(lax.all_gather(w_out, 'seq'), axis=1)]
  transfers between devices with their start and end apart: 6 -> 6, of which waited for: 5 -> 5; matrix products, arithmetic and copies ran while one was open for 13% -> 12% of each run, Pallas kernels for 0% -> 0%
where the time goes in v1:
time: 327 us; the launch traced here: 326 us
  waiting for transfers between devices  162 us (50%)
  blocking collectives  65.4 us (20%)
  other arithmetic  39.7 us (12%)
  local copies, waits for them, and re-layouts  21.6 us (7%)
  between operations  13.4 us (4%)
  matrix products  12.6 us (4%)
  starting transfers between devices  11.1 us (3%)
    all_gather x1, waiting for transfers between devices, per_device(): lax.all_gather(w_query, 'seq', axis=0, tiled=True)  66.9 us
    all_gather x1, waiting for transfers between devices, per_device(): lax.all_gather(w_out, 'seq')  41.9 us
    all_gather x1, blocking collectives, per_device(): key_rows = lax.all_gather(keys_all, 'seq', axis=0, tiled=True)  33.3 us
    all_gather x1, blocking collectives, per_device(): value_rows = lax.all_gather(values, 'seq', axis=0, tiled=True)  32.1 us
    all_to_all x1, waiting for transfers between devices, per_device(): lax.all_to_all(outgoing, 'seq', split_axis=0, concat_axis=0, tiled=True)  28.1 us
    all_to_all x1, waiting for transfers between devices, per_device(): lax.all_to_all(outgoing_back, 'seq', split_axis=0, concat_axis=0, tiled=T...  14.8 us
    scatter-add x1, other arithmetic, per_device(): mixed = tokens.astype(jnp.float32).at[spot_row].add(lift_rows, mode='drop')  13.8 us
    all_gather x1, waiting for transfers between devices, per_device(): lax.all_gather(w_key, 'seq', axis=0, tiled=True)  7.52 us
  transfers between devices with their start and end apart: 6, of which 5 were waited for; matrix products, arithmetic and copies ran while one was open for 12% of the time, Pallas kernels for 0%

profile of v1, /device:TPU:0, one launch (start us, length us, event | category | flops | bytes accessed | tf_op | source)
XLA Modules:
  0.0 325.8 jit_solution(380117726166880226)
XLA Ops:
  6.5 0.7 all-gather.10.cloned.1.call-update
  7.3 0.0 all-gather.6.cloned.1.call-start
  7.3 0.7 all-gather.6.cloned.1.call-update
  8.1 0.7 all-gather.12.cloned.1.call-update
  8.8 0.5 all-gather.8.cloned.1.call-update
  9.3 0.7 add_select_fusion.3
  10.0 0.1 convert_reduce_fusion
  10.1 0.6 dynamic_slice.26
  10.7 0.2 reduce-window.7
  10.9 0.7 fusion.43
  11.6 0.6 and_select_fusion.3
  12.3 0.7 add_compare_fusion.1
  12.9 0.1 lt.196
  13.0 0.7 fusion.23
  13.7 0.1 min.34
  13.8 1.4 gather_fusion.2
  15.2 5.1 %gather_fusion.3 = bf16[256,2048]{1,0:T(8,128)(2,1)S(1)} fusion(bf16[1024,2048]{1,0:T(8,128)(2,1)} %param.9, s32[1024]{0:T(1024)S(1)} %pad_clamp_fusion.4), kind=kCustom, calls=%fused_computation.3 | custom fusion | bytes 2098176 | tf_op jit(solution)/shard_map/gather | solution.py:45
  20.3 0.3 multiply_reduce_fusion
  20.6 0.1 rsqrt.12
  20.7 1.3 fusion.21
  22.0 7.3 %all-to-all-start = ((bf16[8,32,2048]{2,1,0:T(8,128)(2,1)}), bf16[8,32,2048]{2,1,0:T(8,128)(2,1)S(1)}, u32[]{:S(2)}, u32[]{:S(2)}) async-start(bf16[8,32,2048]{2,1,0:T(8,128)(2,1)} %fusion.21), calls=%async_computation | async-start | bytes 2097152 | tf_op jit(solution)/shard_map/all_to_all | solution.py:49
  29.3 1.0 gather_fusion.4
  30.3 0.1 compare_select_fusion
  30.4 0.1 reshape.718
  30.5 4.9 %fusion.40 = s32[128]{0:T(128)S(1)} fusion(s32[128]{0:T(128)S(1)} %gather_fusion.4, s32[]{:T(128)} %bitcast.16, s32[]{:T(128)} %bitcast.17, s32[]{:T(128)} %bitcast.18, s32[]{:T(128)} %bitcast.19, s32[]{:T(128)} %bitcast.20, s32[]{:T(128)} %bitcast.22, s32[]{:T(128)} %bitcast.21, s32[]{:T(128)} %bitcast.15, s32[]{:T(128)} %axis_index.12), kind=kLoop, calls=%fused_computation.132 | loop fusion | flops 5120 | bytes 1060 | tf_op jit(solution)/shard_map/select_n | solution.py:54
  35.5 28.1 %all-to-all-done = bf16[8,32,2048]{2,1,0:T(8,128)(2,1)S(1)} async-done(((bf16[8,32,2048]{2,1,0:T(8,128)(2,1)}), bf16[8,32,2048]{2,1,0:T(8,128)(2,1)S(1)}, u32[]{:S(2)}, u32[]{:S(2)}) %all-to-all-start) | async-done | bytes 1048608 | tf_op jit(solution)/shard_map/all_to_all | solution.py:49
  63.5 0.9 gather_fusion.5
  64.5 1.5 convolution_convert_fusion.1
  66.0 32.1 %all_gather.25 = bf16[1024,256]{1,0:T(8,128)(2,1)S(1)} all-gather(bf16[128,256]{1,0:T(8,128)(2,1)S(1)} %convolution_convert_fusion.1), channel_id=1, replica_groups=mesh['dp'=4,'seq'=8] {'seq'}, dimensions={0}, use_global_device_ids=true | all-gather | bytes 589824 | tf_op jit(solution)/shard_map/all_gather | solution.py:81
  98.2 7.5 %all-gather.6.cloned.1.call-done = bf16[2048,256]{1,0:T(8,128)(2,1)} async-done(((bf16[256,256]{1,0:T(8,128)(2,1)}), bf16[2048,256]{1,0:T(8,128)(2,1)}) %all-gather.6.cloned.1.call-update) | async-done | bytes 1048592 | tf_op jit(solution)/shard_map/all_gather | solution.py:62
  105.7 1.5 convolution_convert_fusion.2
  107.2 33.3 %all_gather.22 = bf16[1024,256]{1,0:T(8,128)(2,1)S(1)} all-gather(bf16[128,256]{1,0:T(8,128)(2,1)S(1)} %convolution_convert_fusion.2), channel_id=1, replica_groups=mesh['dp'=4,'seq'=8] {'seq'}, dimensions={0}, use_global_device_ids=true | all-gather | bytes 589824 | tf_op jit(solution)/shard_map/all_gather | solution.py:80
  140.5 41.9 %all-gather.12.cloned.1.call-done = bf16[8192,256]{1,0:T(8,128)(2,1)} async-done(((bf16[1024,256]{1,0:T(8,128)(2,1)}), bf16[8192,256]{1,0:T(8,128)(2,1)}) %all-gather.12.cloned.1.call-update) | async-done | bytes 4194320 | tf_op jit(solution)/shard_map/all_gather | solution.py:120
  182.5 6.4 %copy.32 = bf16[1024,8,256]{0,2,1:T(8,128)(2,1)} copy(bf16[1024,8,256]{2,0,1:T(8,128)(2,1)} %bitcast.127) | data formatting | bytes 8388608 | tf_op jit(solution)/shard_map/reshape | solution.py:120
  188.9 66.9 %all-gather.8.cloned.1.call-done = bf16[2048,1024]{1,0:T(8,128)(2,1)} async-done(((bf16[256,1024]{1,0:T(8,128)(2,1)}), bf16[2048,1024]{1,0:T(8,128)(2,1)}) %all-gather.8.cloned.1.call-update) | async-done | bytes 4194320 | tf_op jit(solution)/shard_map/all_gather | solution.py:61
  255.8 2.9 fusion.20
  258.7 0.2 reshape.648
  259.0 4.9 %while.20 = (s32[]{:T(128)}, f32[2,4,128]{2,1,0:T(4,128)S(1)}, f32[2,4,128]{2,1,0:T(4,128)S(1)}, f32[2,4,128,128]{3,2,1,0:T(8,128)S(1)}, bf16[1024,256]{1,0:T(8,...) while((s32[]{:T(128)}, f32[2,4,128]{2,1,0:T(4,128)S(1)}, ...), condition=%wide.region_6.7_spmd.clone, body=%wide.region_3.6_spmd.clone.sunk | while | flops 274153728 | bytes 10556611 | solution.py:112
  259.0 0.1 broadcast_compare_fusion.2
  259.2 0.1 copy.44
  259.3 0.1 copy.45
  259.5 0.5 fusion.68
  260.0 0.4 fusion.69
  260.5 0.9 convolution_add_fusion.2
  261.5 0.1 broadcast_compare_fusion.2
  261.6 0.1 copy.44
  261.8 0.1 copy.45
  261.9 0.5 fusion.68
  262.5 0.4 fusion.69
  262.9 0.9 convolution_add_fusion.2
  263.9 0.2 copy.31
  264.1 0.1 divide_convert_fusion
  264.1 3.7 %convolution_convert_fusion = bf16[128,2048]{1,0:T(8,128)(2,1)S(1)} fusion(bf16[128,1024]{0,1:T(8,128)(2,1)S(1)} %bitcast.128, bf16[1024,2048]{0,1:T(8,128)(2,1)} %bitcast.122), kind=kOutput, calls=%fused_computation.42 | convolution fusion | flops 537133056 | bytes 4980736 | tf_op jit(solution)/shard_map/dot_general | solution.py:118
  267.9 1.4 gather_fusion.6
  269.2 1.1 broadcast_select_fusion
  270.3 3.7 %all-to-all-start.1 = ((bf16[8,32,2048]{2,1,0:T(8,128)(2,1)}), bf16[8,32,2048]{2,1,0:T(8,128)(2,1)S(1)}, u32[]{:S(2)}, u32[]{:S(2)}) async-start(bf16[8,32,2048]{2,1,0:T(8,128)(2,1)} %broadcast_select_fusion), calls=%async_computation.1 | async-start | bytes 2097152 | tf_op jit(solution)/shard_map/all_to_all | solution.py:132
  274.1 6.5 %convert_element_type.56 = f32[1024,2048]{1,0:T(8,128)} convert(bf16[1024,2048]{1,0:T(8,128)(2,1)} %param.9) | non-fusion elementwise | flops 2097152 | bytes 12582912 | tf_op jit(solution)/shard_map/convert_element_type | solution.py:139
  280.6 0.6 compare_select_fusion.1
  281.2 1.4 gather_fusion
  282.6 1.4 gather_fusion.1
  284.0 0.6 compare_select_fusion.4
  284.7 14.8 %all-to-all-done.1 = bf16[8,32,2048]{2,1,0:T(8,128)(2,1)S(1)} async-done(((bf16[8,32,2048]{2,1,0:T(8,128)(2,1)}), bf16[8,32,2048]{2,1,0:T(8,128)(2,1)S(1)}, u32[]{:S(2)}, u32[]{:S(2)}) %all-to-all-start.1) | async-done | bytes 1048608 | tf_op jit(solution)/shard_map/all_to_all | solution.py:132
  299.5 13.8 %scatter_custom_fusion = f32[1024,2048]{1,0:T(8,128)} fusion(f32[1024,2048]{1,0:T(8,128)} %convert_element_type.56, s32[256]{0:T(256)S(1)} %bitcast.136, f32[256]{0:T(256)S(1)} %gather_fusion.1, bf16[256,2048]{1,0:T(8,128)(2,1)S(1)} %bitcast.125, s32[1024]{0:T(1024)S(1)} %pad_clamp_fusion), kind=kCustom, calls=%fused_computation.43 | custom fusion | flops 1572864 | bytes 9442304 | tf_op jit(solution)/shard_map/scatter-add | solution.py:139
  313.2 6.0 %convert_element_type.70 = bf16[1024,2048]{1,0:T(8,128)(2,1)} convert(f32[1024,2048]{1,0:T(8,128)} %scatter_custom_fusion) | non-fusion elementwise | flops 2097152 | bytes 12582912 | tf_op jit(solution)/shard_map/convert_element_type | solution.py:140
  (39 shorter events, 0.4 us)
Async XLA Ops:
  6.5 276.1 %copy-start = (f32[1024]{0:T(1024)S(1)}, f32[1024]{0:T(1024)}, u32[]{:S(2)}) copy-start(f32[1024]{0:T(1024)} %param.11) | copy-start | bytes 12292
  6.5 7.3 %copy-start.1 = (s32[1024]{0:T(1024)S(1)}, s32[1024]{0:T(1024)}, u32[]{:S(2)}) copy-start(s32[1024]{0:T(1024)} %param.10) | copy-start | bytes 12292
  6.5 57.9 %all-gather.10.cloned.1.call-start = ((), (), s32[]{:S(2)}) async-start(), calls=%async_computation.4 | async-start | bytes 1179648 | tf_op jit(solution)/shard_map/all_gather | solution.py:63
  7.3 98.4 %all-gather.6.cloned.1.call-start = ((), (), s32[]{:S(2)}) async-start(), calls=%async_computation.2 | async-start | bytes 1179648 | tf_op jit(solution)/shard_map/all_gather | solution.py:62
  8.0 174.4 %all-gather.12.cloned.1.call-start = ((), (), s32[]{:S(2)}) async-start(), calls=%async_computation.5 | async-start | bytes 4718592 | tf_op jit(solution)/shard_map/all_gather | solution.py:120
  8.7 247.0 %all-gather.8.cloned.1.call-start = ((), (), s32[]{:S(2)}) async-start(), calls=%async_computation.3 | async-start | bytes 4718592 | tf_op jit(solution)/shard_map/all_gather | solution.py:61
  22.0 41.5 %all-to-all-start = ((bf16[8,32,2048]{2,1,0:T(8,128)(2,1)}), bf16[8,32,2048]{2,1,0:T(8,128)(2,1)S(1)}, u32[]{:S(2)}, u32[]{:S(2)}) async-start(bf16[8,32,2048]{2,1,0:T(8,128)(2,1)} %fusion.21), calls=%async_computation | async-start | bytes 2097152 | tf_op jit(solution)/shard_map/all_to_all | solution.py:49
  270.3 29.1 %all-to-all-start.1 = ((bf16[8,32,2048]{2,1,0:T(8,128)(2,1)}), bf16[8,32,2048]{2,1,0:T(8,128)(2,1)S(1)}, u32[]{:S(2)}, u32[]{:S(2)}) async-start(bf16[8,32,2048]{2,1,0:T(8,128)(2,1)} %broadcast_select_fusion), calls=%async_computation.1 | async-start | bytes 2097152 | tf_op jit(solution)/shard_map/all_to_all | solution.py:132
Sparse Core Ops, SparseCore 0:
  9.5 53.3 all-gather.9
  65.0 40.6 all-gather.5
  107.8 74.5 all-gather.11
  184.4 71.3 all-gather.7
